TPU v7x, 128 devices: a whole 4x4x4 slice. The times are simulated.
128 devices in a mesh: rep: 2 (over core), dp: 64 (over x, y, z).
Axes of the slice: x: 4, y: 4, z: 4, core: 2. Of those that a mesh axis runs over, the one named last changes fastest.
Arguments:
- x: bfloat16 [128, 1024, 1280], P(('rep', 'dp')), parts along dimension 0
- dy: bfloat16 [128, 1024, 1280], P(('rep', 'dp')), parts along dimension 0
- w_gate: bfloat16 [2, 1280, 4096], replicated
- w_up: bfloat16 [2, 1280, 4096], replicated
- w_down: bfloat16 [2, 4096, 1280], replicated
- m_w_gate: float32 [2, 1280, 4096], P(None, 'dp')
- m_w_up: float32 [2, 1280, 4096], P(None, 'dp')
- m_w_down: float32 [2, 4096, 1280], P(None, 'dp')
- v_w_gate: float32 [2, 1280, 4096], P(None, 'dp')
- v_w_up: float32 [2, 1280, 4096], P(None, 'dp')
- v_w_down: float32 [2, 4096, 1280], P(None, 'dp')
Outputs:
- output 1: bfloat16 [4, 1280, 4096], P('rep'), parts along dimension 0
- output 2: bfloat16 [4, 1280, 4096], P('rep'), parts along dimension 0
- output 3: bfloat16 [4, 4096, 1280], P('rep'), parts along dimension 0
- output 4: float32 [4, 1280, 4096], P('rep', 'dp'), parts along dimension 0
- output 5: float32 [4, 1280, 4096], P('rep', 'dp'), parts along dimension 0
- output 6: float32 [4, 4096, 1280], P('rep', 'dp'), parts along dimension 0
- output 7: float32 [4, 1280, 4096], P('rep', 'dp'), parts along dimension 0
- output 8: float32 [4, 1280, 4096], P('rep', 'dp'), parts along dimension 0
- output 9: float32 [4, 4096, 1280], P('rep', 'dp'), parts along dimension 0
There are 2 independent parts. A program takes and returns all parts, laid end to end along the dimension named above; an argument that names none is the same for every part.
All inputs are finite; a program needn't handle non-finite values.
Results may differ from a plain program's by a relative error of at most 0.022.
Values are sent between devices in bfloat16 or wider.
A program may use at most 1.5 GiB of HBM per device.

v0:
```python
import jax
import jax.numpy as jnp
from jax import lax
from jax.experimental import pallas as pl
from jax.experimental.pallas import tpu as pltpu
from jax.sharding import PartitionSpec as P

AXES = ("x", "y", "z")
STRIDE = {"x": 16, "y": 4, "z": 1}
ORDERS = (("x", "y", "z"), ("y", "z", "x"), ("z", "x", "y"))
BF, F32 = jnp.bfloat16, jnp.float32
D, FF, TOKENS = 1280, 4096, 1024
ROWS = 3840
U, SUPER = 80, 16

MIDDLE = "DADAAEAAAAA"
CUTS = (5, 9, 14, 18, 21, 24, 25, 27, 28, 31, 32, 36, 39, 42, 44, 46, 49, 53, 56, 60, 61, 62, 63)
LAYER = 24 + len(MIDDLE) + 1
ITEMS = LAYER + 27


def entries():
    rows = {"W": 80, "D": 256, "E": 128}
    items = "PWW" * 8 + MIDDLE + "X" + "PWW" * 8 + "DDE"
    made, steps, step = 0, [], 0
    while len(steps) < SUPER:
        first, last = ((0, *CUTS)[step], CUTS[step]) if step < len(CUTS) else (ITEMS, ITEMS)
        made += sum(rows.get(item, 0) for item in items[first:last])
        if made >= 3 * U * (len(steps) + 1):
            steps.append(step)
        step += 1
    return tuple(steps)


ENTRIES = entries()


def lookup(step, values):
    out = values[0]
    for i in range(1, len(values)):
        if values[i] != values[i - 1]:
            out = out + jnp.where(step >= i, values[i] - values[i - 1], 0)
    return out


def entered(step):
    return sum(jnp.where(step > entry, 1, 0) for entry in ENTRIES)


def dot(a, b, dims):
    return lax.dot_general(a, b, (dims, ((), ())), preferred_element_type=F32)


def loop(n, body, unroll=1):
    lax.fori_loop(0, n, lambda i, _: (body(i), None)[1], None, unroll=unroll)


def start(copies):
    for copy in copies:
        copy.start()


def wait(copies):
    for copy in copies:
        copy.wait()


class Refs:
    def __init__(self, operands, buffers):
        self.x, self.dy, self.wg, self.wu, self.wd, self.h, self.kept = operands
        self.a, self.d, self.ws, self.wds, self.p, self.dgu, self.da, self.out, self.sem = buffers
        self.state = self.p.at[:, FF - D :]

    def slabs(self, i):
        slot, layer = i % 2, (i // 8 + 1) // 2 % 2
        pairs = [(self.wd.at[layer, pl.ds(pl.multiple_of(i % 8 * 512, 512), 512), :], self.wds.at[slot])]
        for n in range(4):
            cols = pl.ds(pl.multiple_of(i % 8 * 512 + n // 2 * 256, 256), 256)
            pairs.append(((self.wg, self.wu)[n % 2].at[layer, :, cols], self.ws.at[slot, :, 256 * n : 256 * n + 256]))
        return [pltpu.make_async_copy(src, dst, self.sem.at[slot, n]) for n, (src, dst) in enumerate(pairs)]

    def next_slabs(self, i):
        wait(self.slabs(i))

        @pl.when(i < 31)
        def _():
            start(self.slabs(i + 1))

    def copy(self, n, src, dst):
        return [pltpu.make_async_copy(src, dst, self.sem.at[n // 6, 5 + n % 6])]

    def load_x(self, part):
        rows = pl.ds(part * TOKENS // 4, TOKENS // 4)
        return [pltpu.make_async_copy(self.x.at[rows, :], self.p.at[rows, FF - D :], self.sem.at[part // 2, 11 + part % 2])]

    def load_dy(self):
        return self.copy(1, self.dy, self.d)

    def keep_h(self):
        return self.copy(2, self.state, self.h)

    def back_h(self):
        return self.copy(3, self.h, self.state)

    def load_a(self):
        return self.copy(4, self.x, self.a)

    def keep(self, f):
        return self.copy(5 + f % 2, self.dgu.at[f % 2], self.kept.at[f])

    def back(self, f):
        return self.copy(7 + f % 2, self.kept.at[f], self.dgu.at[f % 2])

    def put(self, g, row, n, at=0, sem=0):
        return self.copy(9 + sem, self.out.at[:, :, :, pl.ds(pl.multiple_of(at, 16), n), :], g.at[:, :, :, pl.ds(pl.multiple_of(row, 16), n), :])


def normed(h):
    wide = h.astype(F32)
    return (wide * lax.rsqrt(jnp.mean(wide * wide, -1, keepdims=True) + 1e-6)).astype(BF)


def token_blocks(size, body):
    loop(TOKENS // size, lambda t: body(pl.ds(pl.multiple_of(t * size, size), size)))


def add_to(ref, rows, cols, first, more):
    ref[rows, cols] = jnp.where(first, more, ref[rows, cols] + more)


PARTS = (
    (slice(0, TOKENS), slice(0, 1024)),
    (slice(0, TOKENS // 2), slice(1024, D)),
    (slice(TOKENS // 2, TOKENS), slice(1024, D)),
)


def gate_and_up(r, rows, b, half):
    both = dot(r.a[rows, :], r.ws[b, :, 512 * half : 512 * half + 512], ((1,), (0,)))
    return both[:, :256], both[:, 256:]


def forward(r):
    for part in range(4):
        start(r.load_x(part))
    start(r.slabs(0) + r.load_dy())
    for part in range(4):
        wait(r.load_x(part))

        def norm(n):
            rows = pl.ds(pl.multiple_of(part * TOKENS // 4 + n * 128, 128), 128)
            r.a[rows, :] = normed(r.state[rows, :])

        loop(TOKENS // 512, norm)

    def task(f):
        r.next_slabs(f)
        b = f % 2

        p = []
        for half in range(2):
            gate, up = gate_and_up(r, slice(None), b, half)
            p.append((gate * jax.nn.sigmoid(gate) * up).astype(BF))
        p = jnp.concatenate(p, 1)
        for rows, cols in PARTS:
            add_to(r.da, rows, cols, f == 0, dot(p[rows], r.wds[b, :, cols], ((1,), (0,))))

    loop(8, task)

    def end(rows):
        h = (r.state[rows, :].astype(F32) + r.da[rows, :].astype(BF).astype(F32)).astype(BF)
        r.state[rows, :] = h
        r.a[rows, :] = normed(h)

    token_blocks(128, end)
    start(r.keep_h())
    wait(r.load_dy())


def do_item(r, g, i):
    slot = jnp.where(i >= LAYER, 1, 0)
    at = i - LAYER * slot

    @pl.when(at < 24)
    def _():
        f, part = at // 3, at % 3

        @pl.when(part == 0)
        def _():
            @pl.when(i == 3)
            def _():
                wait(r.keep_h())

            hidden_task(r, slot, f)

        @pl.when(part > 0)
        def _():
            columns_task(r, g, slot, 2 * f + part - 1)

    @pl.when(i == 24)
    def _():
        start(r.load_a())
        wait(r.keep(7))
        start(r.back(0))
        start(r.back(1))

    downs = [at for at, kind in enumerate(MIDDLE) if kind != "A"]
    t = jnp.where(slot == 1, at - 24, sum(jnp.where(at > 24 + d, 1, 0) for d in downs[:2]))
    down = (slot == 1) & (at >= 24)
    for d in downs:
        down = down | ((slot == 0) & (at == 24 + d))

    @pl.when(down & (t < 2))
    def _():
        down_task(r, g, slot, t, 512)

    @pl.when(down & (t == 2))
    def _():
        down_task(r, g, slot, t, 256)

    @pl.when((i >= 24) & (i < LAYER - 1) & jnp.logical_not(down))
    def _():
        da_task(r, at - 24 - sum(jnp.where(at > 24 + d, 1, 0) for d in downs))

    @pl.when(i == LAYER - 1)
    def _():
        next_layer(r)


def item_done(r, g, i):
    slot = jnp.where(i >= LAYER, 1, 0)
    at = i - LAYER * slot
    n = at // 3 * 2 + at % 3 - 1

    for m in range(3):
        @pl.when((at < 24) & (at % 3 > 0) & (n % 3 == m))
        def _():
            wait(r.put(g, 1920 * slot + 80 * n, 80, 80 * m, m))

    downs = [at for at, kind in enumerate(MIDDLE) if kind != "A"]
    for t in range(3):
        @pl.when(((slot == 0) & (at == 24 + downs[t])) | ((slot == 1) & (at == 24 + t)))
        def _():
            wait(r.put(g, 1920 * slot + 1280 + 256 * t, (256, 256, 128)[t]))


def hidden_task(r, slot, f):
    i = 8 + 16 * slot + f
    b = i % 2
    r.next_slabs(i)

    @pl.when((slot == 0) & (f > 0))
    def _():
        wait(r.keep(f - 1))

    def block(rows):
        dp = dot(r.d[rows, :], r.wds[b], ((1,), (1,))).astype(BF).astype(F32)
        for half in range(2):
            gate, up = gate_and_up(r, rows, b, half)
            sig = jax.nn.sigmoid(gate)
            silu = gate * sig
            d = dp[:, 256 * half : 256 * half + 256]
            r.p[rows, pl.ds(pl.multiple_of(f * 512 + 256 * half, 256), 256)] = (silu * up).astype(BF)
            r.dgu[b, rows, 512 * half : 512 * half + 256] = (d * up * (sig * (1 + (gate - silu)))).astype(BF)
            r.dgu[b, rows, 512 * half + 256 : 512 * half + 512] = (d * silu).astype(BF)

    block(slice(None))

    @pl.when(slot == 0)
    def _():
        start(r.keep(f))


def columns_task(r, g, slot, n):
    b, region = n // 2 % 2, n % 3
    cols = pl.ds(pl.multiple_of(n % 2 * 512, 512), 512)

    def gradients(k):
        of_both = dot(r.a[:, k * 640 : k * 640 + 640], r.dgu[b, :, cols], ((0,), (0,)))
        low = lax.broadcasted_iota(jnp.int32, (8, 128), 0) < 4
        for pair in range(16):
            row = 40 * pair
            parts = ([], [])
            for ct in range(2):
                gate, up = (of_both[row : row + 40, at + 128 * ct : at + 128 * ct + 128] for at in (0, 256))
                gm, um = gate[16:24], up[16:24]
                parts[0].extend((gate[:16], up[:16], jnp.where(low, gm, pltpu.roll(um, 4, 0))))
                parts[1].extend((gate[24:], up[24:], jnp.where(low, pltpu.roll(gm, 4, 0), um)))
            for odd in range(2):
                at = (2 * k + pair // 8, pair // 2 % 4, pair % 2 * 2 + odd)
                r.out[at + (pl.ds(pl.multiple_of(80 * region, 16), 80),)] = jnp.concatenate(parts[odd], 0).astype(BF)

    for k in range(2):
        gradients(k)
    for m in range(3):
        @pl.when(region == m)
        def _():
            start(r.put(g, 1920 * slot + 80 * n, 80, 80 * m, m))


def da_task(r, f):
    i = 16 + f
    r.next_slabs(i)
    wait(r.back(f))
    b = i % 2

    for rows, cols in PARTS:
        add_to(r.da, rows, cols, f == 0, dot(r.dgu[b, rows, :], r.ws[b, cols, :], ((1,), (1,))))

    @pl.when(f < 6)
    def _():
        start(r.back(f + 2))


def down_task(r, g, slot, t, width):
    cols = pl.ds(pl.multiple_of(t * 512, 512), width)

    for k in range(4):
        of_down = dot(r.p[:, 1024 * k : 1024 * k + 1024], r.d[:, cols], ((0,), (0,)))
        for ct in range(width // 128):
            part = of_down[:, 128 * ct : 128 * ct + 128].reshape(4, 4, 64, 128).astype(BF)
            r.out[k, :, :, 64 * ct : 64 * ct + 64, :] = part

    start(r.put(g, 1920 * slot + 1280 + 256 * t, width // 2))


def next_layer(r):
    start(r.back_h())
    wait(r.back_h())

    def block(rows):
        wide = r.state[rows, :].astype(F32)
        d = r.da[rows, :].astype(BF).astype(F32)
        scale = lax.rsqrt(jnp.mean(wide * wide, -1, keepdims=True) + 1e-6)
        along = jnp.mean(wide * d, -1, keepdims=True)
        through = (scale * d - wide * (scale * scale * scale) * along).astype(BF)
        r.d[rows, :] = (r.d[rows, :].astype(F32) + through.astype(F32)).astype(BF)

    token_blocks(128, block)
    wait(r.load_a())

    def norm(rows):
        r.a[rows, :] = normed(r.a[rows, :])

    token_blocks(128, norm)


def comm_kernel(r, g, params, moments, wall, moments_out,
                recv1, send2, recv2, own, sa, b1s, b1r, b2s, b2r, sb, c1s, c1r, c2s, c2r,
                gm, gw, gn, rows24, dm, dw, dn, wn, ssem, rsem, ssem2, rsem2, lsem):
    me = lax.axis_index("dp")
    pos = {"x": me // 16, "y": (me // 4) % 4, "z": me % 4}
    low = (U // 2 + 15) // 16 * 16
    halves = (pl.ds(0, 2), pl.ds(2, 2))
    row_halves = (pl.ds(0, low), pl.ds(low, U - low))

    def peer(axis, by):
        return {"dp": me + ((pos[axis] + by) % 4 - pos[axis]) * STRIDE[axis]}

    barrier = pltpu.get_barrier_semaphore()
    for axis in AXES:
        for by in (1, 3):
            pl.semaphore_signal(barrier, inc=1, device_id=peer(axis, by), device_id_type=pl.DeviceIdType.MESH)
    forward(r)
    pl.semaphore_wait(barrier, 6)

    def part(ref, fixed, rows):
        return ref.at[tuple(fixed.get(axis, slice(None)) for axis in AXES) + (rows, slice(None))]

    def remote(kind, slot, c, way, src, dst, axis):
        return pltpu.make_async_remote_copy(
            src_ref=src, dst_ref=dst, send_sem=ssem.at[kind, slot, c, way], recv_sem=rsem.at[kind, slot, c, way],
            device_id=peer(axis, (1, 3)[way]), device_id_type=pl.DeviceIdType.MESH)

    def local(kind, slot, c, src, dst):
        return pltpu.make_async_copy(src, dst, lsem.at[kind, slot, c])

    class Chunk:
        def __init__(self, c, j):
            self.c, self.slot, self.turn = c, j % 2, j % 3
            self.A, self.B, self.C = ORDERS[c]
            self.rest = tuple(axis for axis in AXES if axis != self.A)
            self.ib = self.rest.index(self.B)
            self.rows = pl.ds(pl.multiple_of((3 * j + c) * U, 16), U)
            self.k, self.layer = (3 * j + c) % 24, 1 - (3 * j + c) // 24
            self.a, self.b, self.c3 = (pos[axis] for axis in ORDERS[c])

        def unit(self, b, i):
            return (b, i) if self.ib == 0 else (i, b)

        def row_part(self, rows):
            return pl.ds(self.rows.start + rows.start, rows.size)

        def a1(self):
            s, c = self.slot, self.c
            return [remote(0, s, c, way, part(g, {self.A: (self.a + 2) % 4, self.rest[0]: halves[way]}, self.rows),
                           recv1.at[s, c, halves[way]], self.A) for way in (0, 1)]

        def load2(self):
            s, c = self.slot, self.c
            return [local(way, s, c, part(g, {self.A: (self.a + (1, 3)[way]) % 4}, self.rows), send2.at[s, c, way]) for way in (0, 1)]

        def load_own(self):
            return [local(2, self.slot, self.c, part(g, {self.A: self.a}, self.rows), own.at[self.slot, self.c])]

        def a2(self):
            s, c = self.slot, self.c
            return [remote(1, s, c, way, send2.at[s, c, way], recv2.at[s, c, way], self.A) for way in (0, 1)]

        def b1(self):
            s, c = self.slot, self.c
            return [remote(2, s, c, way, b1s.at[s, c, halves[way]], b1r.at[s, c, halves[way]], self.B) for way in (0, 1)]

        def b2(self):
            s, c = self.slot, self.c
            return [remote(3, s, c, way, b2s.at[s, c, way], b2r.at[s, c, way], self.B) for way in (0, 1)]

        def c1(self):
            s, c = self.slot, self.c
            return [remote(4, s, c, way, c1s.at[s, c, row_halves[way]], c1r.at[s, c, row_halves[way]], self.C) for way in (0, 1)]

        def c2(self):
            s, c = self.slot, self.c
            return [remote(5, s, c, way, c2s.at[s, c, way], c2r.at[s, c, way], self.C) for way in (0, 1)]

        def of_columns(self, out):
            s, c = self.slot, self.c
            cols = pl.ds(pl.multiple_of(self.k * 256, 256), 256)
            pairs = []
            for i in range(4):
                which = i // 2 * 3 + i % 2
                if out:
                    pairs.append((gn.at[s, c, i], moments_out[which].at[self.layer, :, cols]))
                else:
                    pairs.append((moments[which].at[:, :, cols], gm.at[s, c, i]))
            if not out:
                rows = pl.ds(pl.multiple_of(me // 2 * 40, 8), 40)
                pairs += [(params[i].at[self.layer, rows, cols], gw.at[s, c, i]) for i in range(2)]
            return [local((10 if out else 3) + i, s, c, *pair) for i, pair in enumerate(pairs)]

        def of_down(self, out, q):
            s, c = self.slot, self.c
            tile = 5 * (self.k - 16) // 4
            pairs = []
            for n, (first, rows, at) in enumerate(((16 * q, 64 - 16 * q, 0), (0, 16 + 16 * q, 64 - 16 * q))):
                cols = pl.ds(pl.multiple_of((tile + n) * 128, 128), 128)
                there, here = pl.ds(first, rows), pl.ds(at, rows)
                for i in range(2):
                    if out:
                        pairs.append((dn.at[s, c, i, here], moments_out[3 * i + 2].at[self.layer, there, cols]))
                    else:
                        pairs.append((moments[3 * i + 2].at[self.layer, there, cols], dm.at[s, c, i, here]))
                if not out:
                    mine = pl.ds(pl.multiple_of(me * 64 + first, 16), rows)
                    pairs.append((params[2].at[self.layer, mine, cols], dw.at[s, c, here]))
            return [local((10 if out else 3) + i, s, c, *pair) for i, pair in enumerate(pairs)]

        def step_copies(self, out, act):
            @pl.when(self.k < 16)
            def _():
                act(self.of_columns(out))

            for q in range(4):
                @pl.when((self.k >= 16) & (self.k % 4 == q))
                def _():
                    act(self.of_down(out, q))

        def store_new(self):
            mine = part(wall, {self.A: self.a, self.B: self.b, self.C: self.c3}, self.rows)
            return [local(9, self.slot, self.c, wn.at[self.slot, self.c], mine)]

        def gather(self, which):
            s, c = self.slot, self.c
            if which < 2:
                axis, here, fixed, kind = self.C, self.c3, {self.A: self.a, self.B: self.b}, 6
            elif which < 4:
                axis, here, fixed, kind = self.B, self.b, {self.A: self.a}, 8
            else:
                axis, here, fixed, kind = self.A, self.a, {}, 10
            if which == 4:
                blocks = [part(wall, {axis: here, self.rest[0]: halves[way]}, self.rows) for way in (0, 1)]
                return [remote(kind, s, c, way, blocks[way], blocks[way], axis) for way in (0, 1)]
            if which % 2 == 0:
                block = part(wall, fixed | {axis: here}, self.rows)
                src = wn.at[s, c] if which == 0 else block
                return [remote(kind, s, c, way, src, block, axis) for way in (0, 1)]
            out = []
            for way in (0, 1):
                block = fixed | {axis: (here + (3, 1)[way]) % 4}
                rows = self.rows
                if which == 1:
                    rows = self.row_part(row_halves[way])
                elif which == 3:
                    block[self.C] = halves[way]
                else:
                    block[self.rest[0]] = halves[way]
                half = part(wall, block, rows)
                out.append(remote(kind + 1, s, c, way, half, half, axis))
            return out

        def last_halves(self):
            out = []
            for way in (0, 1):
                half = part(wall, {self.A: self.a, self.rest[0]: halves[1 - way]}, self.rows)
                out.append(pltpu.make_async_remote_copy(
                    src_ref=half, dst_ref=half, send_sem=ssem2.at[self.turn, self.c, way], recv_sem=rsem2.at[self.turn, self.c, way],
                    device_id=peer(self.A, (1, 3)[way]), device_id_type=pl.DeviceIdType.MESH))
            return out

    def stage0(k):
        start(k.a1())
        start(k.load2())

    def stage1(k):
        wait(k.load2())
        wait(k.a1())
        s, c = k.slot, k.c

        def body(i):
            for way in (0, 1):
                at = (s, c, 2 * way + i // 4, i % 4)
                to = (s, c, way, 2 * way + i // 4, i % 4)
                send2[to] = (send2[to].astype(F32) + recv1[at].astype(F32)).astype(BF)

        loop(8, body)
        start(k.a2())
        start(k.load_own())

    def stage2(k):
        wait(k.load_own())
        wait(k.a2())
        s, c = k.slot, k.c

        def body(i):
            at = (i // 4, i % 4)
            total = own[(s, c) + at].astype(F32) + recv2[(s, c, 0) + at].astype(F32) + recv2[(s, c, 1) + at].astype(F32)
            sa[(s, c) + at] = total

        loop(16, body)
        far = (k.b + 2) % 4

        def pack(i):
            b1s[s, c, i] = sa[(s, c) + k.unit(far, i)].astype(BF)

        loop(4, pack)
        start(k.b1())

    def stage3(k):
        wait(k.b1())
        s, c = k.slot, k.c
        near = ((k.b + 1) % 4, (k.b + 3) % 4)

        def body(i):
            for way in (0, 1):
                b2s[s, c, way, 2 * way + i] = (sa[(s, c) + k.unit(near[way], 2 * way + i)] + b1r[s, c, 2 * way + i].astype(F32)).astype(BF)
                b2s[s, c, way, 2 - 2 * way + i] = sa[(s, c) + k.unit(near[way], 2 - 2 * way + i)].astype(BF)

        loop(2, body)
        start(k.b2())

    def stage4(k):
        wait(k.b2())
        s, c = k.slot, k.c

        def body(i):
            sb[s, c, i] = sa[(s, c) + k.unit(k.b, i)] + b2r[s, c, 0, i].astype(F32) + b2r[s, c, 1, i].astype(F32)

        loop(4, body)
        c1s[s, c] = sb[s, c, (k.c3 + 2) % 4].astype(BF)
        start(k.c1())

    def stage5(k):
        wait(k.c1())
        s, c = k.slot, k.c
        near = ((k.c3 + 1) % 4, (k.c3 + 3) % 4)
        for way in (0, 1):
            add, keep = row_halves[way], row_halves[1 - way]
            c2s[s, c, way, add] = (sb[s, c, near[way], add] + c1r[s, c, add].astype(F32)).astype(BF)
            c2s[s, c, way, keep] = sb[s, c, near[way], keep].astype(BF)
        start(k.c2())
        k.step_copies(False, start)

    def adamw(old, first, second, grad):
        first = 0.9 * first + 0.1 * grad
        second = 0.95 * second + 0.05 * grad * grad
        return old - 0.02 * (first * lax.rsqrt(second + 1e-8) + 0.1 * old), first, second

    def step_columns(k, grad):
        s, c = k.slot, k.c
        low = lax.broadcasted_iota(jnp.int32, (8, 128), 0) < 4
        odd = me % 2 == 1
        unit = []
        for ct in range(2):
            tile = slice(128 * ct, 128 * ct + 128)
            mix = grad[40 * ct + 32 : 40 * ct + 40]
            turned = pltpu.roll(mix, 4, 0)
            whole, left = [], []
            for i in range(2):
                rest = jnp.where(odd, (turned, mix)[i], (mix, turned)[i])
                rows = jnp.concatenate([grad[40 * ct + 16 * i : 40 * ct + 16 * i + 16], rest], 0)
                rows = jnp.where(odd, pltpu.roll(rows, 4, 0), rows)
                pair = gw[s, c, i, :, tile].astype(F32)
                old = jnp.where(odd, pltpu.roll(pair[16:40], 20, 0), pair[0:24])
                first, second = (jnp.where(k.layer == 1, gm[s, c, n, :, 1, tile], gm[s, c, n, :, 0, tile]) for n in (i, 2 + i))
                new, first, second = adamw(old[:20], first, second, rows[:20])
                gn[s, c, i, :, tile] = first
                gn[s, c, 2 + i, :, tile] = second
                rows24[ct, i, 0:20] = new
                new = rows24[ct, i]
                new = jnp.where(odd, pltpu.roll(new, 20, 0), new)
                whole.append(new[:16])
                turn = pltpu.roll(new[16:], 4, 0)
                left.append(jnp.where(odd, (turn, new[16:])[i], (new[16:], turn)[i]))
            unit += whole + [jnp.where(low, *left)]
        wn[s, c] = jnp.concatenate(unit, 0).astype(BF)

    def stage6(k):
        k.step_copies(False, wait)
        wait(k.c2())
        s, c = k.slot, k.c
        total = sb[s, c, k.c3] + c2r[s, c, 0].astype(F32) + c2r[s, c, 1].astype(F32)
        grad = total.astype(BF).astype(F32)

        @pl.when(k.k < 16)
        def _():
            step_columns(k, grad)

        @pl.when(k.k >= 16)
        def _():
            new, dn[s, c, 0], dn[s, c, 1] = adamw(dw[s, c].astype(F32), dm[s, c, 0], dm[s, c, 1], grad)
            wn[s, c] = new.astype(BF)

        start(k.gather(0))
        start(k.store_new())
        k.step_copies(True, start)

    def stage7(k):
        wait(k.gather(0))
        start(k.gather(1))

    def stage8(k):
        wait(k.store_new())
        k.step_copies(True, wait)
        wait(k.gather(1))
        start(k.gather(2))

    def later(n):
        def stage(k):
            wait(k.gather(n - 1))
            start(k.gather(n))
            if n == 4:
                start(k.last_halves())
        return stage

    def stage12(k):
        wait(k.gather(5))
        wait(k.last_halves())

    stages = (stage0, stage1, stage2, stage3, stage4, stage5, stage6, stage7, stage8, later(3), later(4), later(5), stage12)

    def step(now):
        first, last = lookup(now, (0, *CUTS)), lookup(now, CUTS)
        lax.fori_loop(first, last, lambda i, _: do_item(r, g, i), None)
        before = [entered(now + 1 - k) for k in range(len(stages) + 1)]
        for number in reversed(range(len(stages))):
            if number == 0:
                lax.fori_loop(first, last, lambda i, _: item_done(r, g, i), None)

            @pl.when(before[number] > before[number + 1])
            def _():
                for c in range(3):
                    stages[number](Chunk(c, before[number + 1]))

    loop(ENTRIES[-1] + len(stages), step)


def whole_kernel(*refs):
    (x, dy), params, moments = refs[:2], refs[2:5], refs[5:11]
    wall, moments_out, g, kept = refs[11], refs[12:18], refs[18], refs[19:21]
    scratch, n = refs[21:], COMM_SCRATCH
    comm_kernel(Refs((x, dy, *params, *kept), scratch[n:]), g, params, moments, wall, moments_out, *scratch[:n])


COMM_SCRATCH = 27


def whole_step(x, dy, params, moments):
    hbm = pl.BlockSpec(memory_space=pl.ANY)
    V, two = pltpu.VMEM, (2, 3)
    comm_scratch = [
        V(two + (4, 4, U, 128), BF), V(two + (2, 4, 4, U, 128), BF), V(two + (2, 4, 4, U, 128), BF), V(two + (4, 4, U, 128), BF),
        V(two + (4, 4, U, 128), F32),
        V(two + (4, U, 128), BF), V(two + (4, U, 128), BF), V(two + (2, 4, U, 128), BF), V(two + (2, 4, U, 128), BF), V(two + (4, U, 128), F32),
        V(two + (U, 128), BF), V(two + (U, 128), BF), V(two + (2, U, 128), BF), V(two + (2, U, 128), BF),
        V(two + (4, 20, 2, 256), F32), V(two + (2, 40, 256), BF), V(two + (4, 20, 256), F32), V((2, 2, 24, 128), F32),
        V(two + (2, U, 128), F32), V(two + (U, 128), BF), V(two + (2, U, 128), F32), V(two + (U, 128), BF),
        pltpu.SemaphoreType.DMA((12, 2, 3, 2)), pltpu.SemaphoreType.DMA((12, 2, 3, 2)), pltpu.SemaphoreType.DMA((3, 3, 2)), pltpu.SemaphoreType.DMA((3, 3, 2)), pltpu.SemaphoreType.DMA((14, 2, 3)),
    ]
    assert len(comm_scratch) == COMM_SCRATCH
    task_scratch = [
        V((TOKENS, D), BF), V((TOKENS, D), BF), V((2, D, 1024), BF), V((2, 512, D), BF),
        V((TOKENS, FF), BF), V((2, TOKENS, 1024), BF), V((TOKENS, D), F32), V((4, 4, 4, 256, 128), BF), pltpu.SemaphoreType.DMA((2, 13)),
    ]
    units = jax.ShapeDtypeStruct((4, 4, 4, ROWS, 128), BF)
    outs = pl.pallas_call(
        whole_kernel,
        out_shape=(units, *(jax.ShapeDtypeStruct((2, t.size // (2 * t.shape[-1]), t.shape[-1]), F32) for t in moments), units, jax.ShapeDtypeStruct(x.shape, BF), jax.ShapeDtypeStruct((8, TOKENS, 1024), BF)),
        in_specs=[hbm] * 11,
        out_specs=(hbm,) * 10,
        scratch_shapes=comm_scratch + task_scratch,
        compiler_params=pltpu.CompilerParams(collective_id=0, has_side_effects=True, vmem_limit_bytes=67043328),
        name="whole_step",
    )(x, dy, *params, *moments)
    return outs[0].reshape(64, ROWS, 128), outs[1:7]


UNPACK, SLOTS = 4, 4


def unpack_kernel(wall, *refs):
    ins, (gate, up, down), outs = refs[:6], refs[6:9], refs[9:15]
    buf, gate_buf, up_buf, down_buf, turn, turned, plain, sem, moment_sem = refs[15:]
    low = lax.broadcasted_iota(jnp.int32, (8, 128), 0) < 4
    blocks = 64 // UNPACK

    def load(i):
        rows = pl.ds(pl.multiple_of(i // blocks * (ROWS // 2), 128), ROWS // 2)
        return [pltpu.make_async_copy(wall.at[pl.ds(i % blocks * UNPACK, UNPACK), rows, :], buf.at[i % SLOTS], sem.at[0, i % SLOTS])]

    def store(i):
        copies = []
        for n, (src, dst) in enumerate(((gate_buf, gate), (up_buf, up), (down_buf, down))):
            rows = src.shape[1]
            there = dst.at[1 - i // blocks, pl.ds(pl.multiple_of(i % blocks * rows, 16), rows), :]
            copies.append(pltpu.make_async_copy(src.at[i % SLOTS], there, sem.at[1 + n, i % SLOTS]))
        return copies

    def moments(out):
        copies = []
        for n in range(6):
            if n % 3 == 2:
                pair = (plain.at[n // 3], outs[n]) if out else (ins[n], plain.at[n // 3])
            else:
                pair = (turned.at[n // 3 * 2 + n % 3], outs[n]) if out else (ins[n], turn.at[n // 3 * 2 + n % 3])
            copies.append(pltpu.make_async_copy(*pair, moment_sem.at[n]))
        return copies

    for i in range(SLOTS - 1):
        start(load(i))
    start(moments(False))

    def block(i):
        slot = i % SLOTS
        wait(load(i))

        @pl.when(i + SLOTS - 1 < 2 * blocks)
        def _():
            start(load(i + SLOTS - 1))

        @pl.when(i >= SLOTS)
        def _():
            wait(store(i - SLOTS))

        for d in range(UNPACK):
            for ct in range(10):
                down_buf[slot, 64 * d : 64 * d + 64, ct * 128 : ct * 128 + 128] = buf[slot, d, 1280 + 64 * ct : 1344 + 64 * ct, :]

        def slab(n):
            rows = pl.ds(pl.multiple_of(80 * n, 16), 80)
            units = [buf[slot, d, rows, :].astype(F32) for d in range(UNPACK)]
            for ct in range(2):
                own = [u[40 * ct : 40 * ct + 40] for u in units]
                tile = pl.ds(pl.multiple_of(n * 256 + ct * 128, 128), 128)
                for which, out in enumerate((gate_buf, up_buf)):
                    parts = []
                    for even, odd in zip(own[::2], own[1::2], strict=True):
                        left, right = even[32:40], odd[32:40]
                        if which == 0:
                            right = pltpu.roll(right, 4, 0)
                        else:
                            left = pltpu.roll(left, 4, 0)
                        parts += [even[16 * which : 16 * which + 16], jnp.where(low, left, right), odd[16 * which : 16 * which + 16]]
                    out[slot, :, tile] = jnp.concatenate(parts, 0).astype(BF)

        loop(16, slab)
        start(store(i))

        @pl.when(i == blocks)
        def _():
            wait(moments(False))
            for n in range(4):
                for layer in range(2):
                    turned[n, :, layer, :] = turn[n, layer]
            start(moments(True))

    loop(2 * blocks, block)
    for i in range(2 * blocks - SLOTS, 2 * blocks):
        wait(store(i))
    wait(moments(True))


def unpack(wall, moments):
    shapes = ((2, D, FF), (2, D, FF), (2, FF, D))
    new = [t.shape if n % 3 == 2 else (t.shape[1], 2, t.shape[2]) for n, t in enumerate(moments)]
    hbm, V = pl.BlockSpec(memory_space=pl.ANY), pltpu.VMEM
    rows = [s[1] // 64 * UNPACK for s in shapes]
    return pl.pallas_call(
        unpack_kernel,
        out_shape=[jax.ShapeDtypeStruct(s, BF) for s in shapes] + [jax.ShapeDtypeStruct(s, F32) for s in new],
        in_specs=[hbm] * 7,
        out_specs=[hbm] * 9,
        scratch_shapes=[
            V((SLOTS, UNPACK, ROWS // 2, 128), BF), *(V((SLOTS, n, s[2]), BF) for n, s in zip(rows, shapes, strict=True)),
            V((4, *moments[0].shape), F32), V((4, *new[0]), F32), V((2, *moments[2].shape), F32),
            pltpu.SemaphoreType.DMA((4, SLOTS)), pltpu.SemaphoreType.DMA((6,)),
        ],
        compiler_params=pltpu.CompilerParams(vmem_limit_bytes=67043328),
        cost_estimate=pl.CostEstimate(flops=10**6, bytes_accessed=142 * 10**6, transcendentals=0),
        name="unpack",
    )(wall, *moments)


def solution(mesh):
    def step(x, dy, *arrays):
        turned = [t if n % 3 == 2 else t.transpose(1, 0, 2) for n, t in enumerate(arrays[3:])]
        out = unpack(*whole_step(x[0], dy[0], arrays[:3], turned))
        return (*out[:3], *(t if n % 3 == 2 else t.transpose(1, 0, 2) for n, t in enumerate(out[3:])))

    seq, whole, rows = P(("rep", "dp")), P(), P(None, "dp", None)
    return jax.shard_map(
        step,
        mesh=mesh,
        in_specs=(seq, seq) + (whole,) * 3 + (rows,) * 6,
        out_specs=(P("rep"),) * 3 + (P("rep", "dp", None),) * 6,
        check_vma=False,
    )
```

profile of v0, /device:TPU:0, one launch (start us, length us, event | category | flops | bytes accessed | tf_op | source)
XLA Modules:
  0.0 571.5 jit_solution(13548868195358013516)
XLA Ops:
  0.6 525.8 %whole_step.1 = (bf16[4,4,4,3840,128]{4,3,2,1,0:T(8,128)(2,1)}, f32[2,20,4096]{2,1,0:T(8,128)}, f32[2,20,4096]{2,1,0:T(8,128)}, f32[2,64,1280]{2,1,0:T(8,128)}, ...) custom-call(bf16[1024,1280]{1,0:T(8,128)(2,1)} %bitcast.12, ...), custom_call_target="tpu_custom_call" | custom-call | tf_op jit(solution)/shard_map/whole_step/pallas_call | solution.py:705
  526.4 44.9 %unpack.1 = (bf16[2,1280,4096]{2,1,0:T(8,128)(2,1)}, bf16[2,1280,4096]{2,1,0:T(8,128)(2,1)}, bf16[2,4096,1280]{2,1,0:T(8,128)(2,1)}, f32[20,2,4096]{2,1,0:T(2,12...) custom-call(bf16[64,3840,128]{2,1,0:T(8,128)(2,1)} %bitcast.11, ...), custom_call_target="tpu_custom_call" | custom-call | flops 1000000 | bytes 142000000 | tf_op jit(solution)/shard_map/unpack/pallas_call | solution.py:807
where the time goes:
time: 572 us; the launch traced here: 571 us
  Pallas kernels  571 us (100%)
    pallas_call x1, Pallas kernels, whole_step(): pl.pallas_call(whole_kernel, out_shape=(units, *(jax.ShapeDtypeStruct((2,...  526 us
    pallas_call x1, Pallas kernels, unpack(): pl.pallas_call(unpack_kernel, out_shape=[jax.ShapeDtypeStruct(s, BF) for...  44.9 us

commit v1 on v0

--- a/solution.py
+++ b/solution.py
@@ -264,7 +264,8 @@
             r.dgu[b, rows, 512 * half : 512 * half + 256] = (d * up * (sig * (1 + (gate - silu)))).astype(BF)
             r.dgu[b, rows, 512 * half + 256 : 512 * half + 512] = (d * silu).astype(BF)
 
-    block(slice(None))
+    for t in range(2):
+        block(slice(TOKENS // 2 * t, TOKENS // 2 * (t + 1)))
 
     @pl.when(slot == 0)
     def _():
@@ -714,7 +715,7 @@
     return outs[0].reshape(64, ROWS, 128), outs[1:7]
 
 
-UNPACK, SLOTS = 4, 4
+UNPACK, SLOTS = 4, 6
 
 
 def unpack_kernel(wall, *refs):

time: 572 us -> 571 us (level)
  no operation moved by 1% of the time
where the time goes in v1:
time: 571 us
  Pallas kernels  570 us (100%)
    pallas_call x1, Pallas kernels, whole_step(): pl.pallas_call(whole_kernel, out_shape=(units, *(jax.ShapeDtypeStruct((2,...  525 us
    pallas_call x1, Pallas kernels, unpack(): pl.pallas_call(unpack_kernel, out_shape=[jax.ShapeDtypeStruct(s, BF) for...  44.5 us

profile of v1, /device:TPU:0, one launch (start us, length us, event | category | flops | bytes accessed | tf_op | source)
XLA Modules:
  0.0 570.5 jit_solution(9618679032396676428)
XLA Ops:
  0.6 525.2 %whole_step.1 = (bf16[4,4,4,3840,128]{4,3,2,1,0:T(8,128)(2,1)}, f32[2,20,4096]{2,1,0:T(8,128)}, f32[2,20,4096]{2,1,0:T(8,128)}, f32[2,64,1280]{2,1,0:T(8,128)}, ...) custom-call(bf16[1024,1280]{1,0:T(8,128)(2,1)} %bitcast.12, ...), custom_call_target="tpu_custom_call" | custom-call | tf_op jit(solution)/shard_map/whole_step/pallas_call | solution.py:706
  525.9 44.5 %unpack.1 = (bf16[2,1280,4096]{2,1,0:T(8,128)(2,1)}, bf16[2,1280,4096]{2,1,0:T(8,128)(2,1)}, bf16[2,4096,1280]{2,1,0:T(8,128)(2,1)}, f32[20,2,4096]{2,1,0:T(2,12...) custom-call(bf16[64,3840,128]{2,1,0:T(8,128)(2,1)} %bitcast.11, ...), custom_call_target="tpu_custom_call" | custom-call | flops 1000000 | bytes 142000000 | tf_op jit(solution)/shard_map/unpack/pallas_call | solution.py:808
